TPU v7x, 32 devices: a whole 2x2x4 slice. The times are simulated.
32 devices in a mesh: chain: 32 (over z, y, x, core).
Axes of the slice: x: 2, y: 2, z: 4, core: 2. Of those that a mesh axis runs over, the one named last changes fastest.
Arguments:
- right_side: float32 [8, 4096], P(None, 'chain'), may hold values from -6 to 6
- diag_block: float32 [8, 8, 4096], P(None, None, 'chain'), may hold values from -2 to 2
- below_block: float32 [8, 8, 4096], P(None, None, 'chain'), may hold values from -2 to 2
- above_block: float32 [8, 8, 4096], P(None, None, 'chain'), may hold values from -2 to 2
- lower_level: float32 [12, 8, 8, 4096], P(None, None, None, 'chain'), may hold values from -0.5 to 0.5
- upper_level: float32 [12, 8, 8, 4096], P(None, None, None, 'chain'), may hold values from -0.5 to 0.5
- final_block: float32 [8, 8, 4096], P(None, None, 'chain'), may hold values from -1 to 1
Outputs:
- basis: float32 [4, 8, 4096], P(None, None, 'chain')
- hess: float32 [4, 3], replicated
All inputs are finite; a program needn't handle non-finite values.
Results may differ from a plain program's by a relative error of at most 0.0001.
Values sent between devices are 32-bit elements; how exact they have to be, the bound alone decides.
No kernel may reach another device: no remote copies, remote signals or barrier semaphores. Data moves between devices by JAX's collectives and lax.ppermute only.
A program may use at most 64 MiB of HBM per device.

v0:
```python
import functools

import jax
import jax.numpy as jnp
from jax import lax
from jax.experimental import pallas as pl
from jax.experimental.pallas import tpu as pltpu
from jax.sharding import PartitionSpec as P


ITERS = 3


EPS = 1e-06
AXIS = "chain"
SUB = 8


def padded_2(x, sides, width):
    for axis, dim in sides:
        peers, length = (lax.axis_size(axis), x.shape[dim])
        up = [(i, (i + 1) % peers) for i in range(peers - 1)]
        down = [(j, i) for i, j in up]
        last = lax.slice_in_dim(x, length - width, length, axis=dim)
        initial = lax.slice_in_dim(x, 0, width, axis=dim)
        before = lax.ppermute(last, axis, up)
        after = lax.ppermute(initial, axis, down)
        x = jnp.concatenate([before, x, after], axis=dim)
    return x


def from_behind(x, axis, by):
    peers = lax.axis_size(axis)
    pairs = [(i, i + by) for i in range(peers) if 0 <= i + by < peers]
    return lax.ppermute(x, axis, pairs)


def blockmul(blocks, field):
    return jnp.einsum("abi,bi->ai", blocks, field, precision=lax.Precision.HIGHEST)


def general(
    right_side, diag_block, below_block, above_block, lower_level, upper_level, final_block
):
    rows_here = right_side.shape[1]
    devices = lax.axis_size("chain")
    whole = rows_here * devices
    count = right_side.shape[0] * whole
    depth = lower_level.shape[0]
    near = [level for level in range(depth) if 2**level < rows_here]
    far = [level for level in range(depth) if 2**level >= rows_here and 2**level < whole]
    reach = sum((2**level for level in near))
    stacked_coef = jnp.concatenate([lower_level[: len(near)], upper_level[: len(near)]], 0)
    wide_coef = padded_2(stacked_coef, (("chain", 3),), reach)
    start_sum = lax.psum(jnp.sum(right_side * right_side), "chain")
    basis = [right_side / jnp.sqrt(start_sum / count + EPS)]
    hess = jnp.zeros((ITERS + 1, ITERS), jnp.float32)
    for column in range(ITERS):
        precondition_field = basis[column]
        current = padded_2(precondition_field, (("chain", 1),), reach)
        offset = 0
        for position in range(len(near)):
            stride = 2 ** near[position]
            length = current.shape[1]
            first_col = offset + stride
            last_col = offset + length - stride
            low_coef = wide_coef[position][:, :, first_col:last_col]
            high_coef = wide_coef[len(near) + position][:, :, first_col:last_col]
            current = (
                current[:, stride : length - stride]
                + blockmul(low_coef, current[:, : length - 2 * stride])
                + blockmul(high_coef, current[:, 2 * stride :])
            )
            offset = first_col
        precondition_field = current
        for precondition_level in far:
            hops = 2**precondition_level // rows_here
            below_rows = from_behind(precondition_field, "chain", hops)
            above_rows = from_behind(precondition_field, "chain", -hops)
            precondition_field = (
                precondition_field
                + blockmul(lower_level[precondition_level], below_rows)
                + blockmul(upper_level[precondition_level], above_rows)
            )
        field = precondition_field + blockmul(final_block, precondition_field)
        padded = padded_2(field, (("chain", 1),), 1)
        result = 2.0 * field + blockmul(diag_block, field)
        result = result + blockmul(below_block, padded[:, :rows_here])
        vector = result + blockmul(above_block, padded[:, 2:])
        stacked = jnp.stack(basis)
        local_dots = jnp.einsum("kai,ai->k", stacked, vector, precision=lax.Precision.HIGHEST)
        dots = lax.psum(local_dots, "chain") / count
        vector = vector - jnp.einsum("k,kai->ai", dots, stacked, precision=lax.Precision.HIGHEST)
        squares = lax.psum(jnp.sum(vector * vector), "chain") / count
        length = jnp.sqrt(squares + EPS)
        basis.append(vector / length)
        hess = hess.at[: column + 1, column].set(dots).at[column + 1, column].set(length)
    return (jnp.stack(basis), hess)


class Plan:
    def __init__(self, devices, rows, depth):
        self.devices, self.rows, self.depth = devices, rows, depth
        self.piece = rows // devices
        self.near = [k for k in range(depth) if 2**k < rows]
        self.far = [k for k in range(depth) if rows <= 2**k < rows * devices]
        self.sent = len(self.near) - 1
        self.count = SUB * rows * devices
        n = len(self.far) - 1
        self.halo_mats = 2 * n + 2
        self.own_mats = self.halo_mats + 3
        self.own_tiles = self.own_mats * SUB
        self.halo_tiles = self.halo_mats * SUB
        self.coef_tiles = self.own_tiles + self.halo_tiles // self.piece
        self.per_group = rows // SUB
        self.groups = -(-self.coef_tiles // self.per_group)
        self.early = -(-self.halo_tiles // self.per_group)
        self.early_rows = self.early * self.piece
        self.late_rows = (self.groups - self.early) * self.piece + 1
        self.width = rows // self.piece


def fits(devices, rows, block, lanes=128):
    piece = rows // devices
    return block == SUB and rows == lanes and piece >= 1 and piece * devices == rows and rows // piece >= 4 * SUB


def lane(shape=(SUB, 128)):
    return lax.broadcasted_iota(jnp.int32, shape, 1)


def sub(shape=(SUB, 128)):
    return lax.broadcasted_iota(jnp.int32, shape, 0)


def spread(v, b):
    return jnp.broadcast_to(v[b : b + 1, :], v.shape)


def added(terms):
    while len(terms) > 1:
        terms = [x + y for x, y in zip(terms[::2], terms[1::2])]
    return terms[0]


def total(x):
    return jnp.sum(jnp.sum(x, axis=0, keepdims=True), axis=1, keepdims=True)


def send(plan, tiles, z_ref, wrap=False, row=None, sums=None):
    q, r = plan.piece, plan.rows
    n = plan.width - SUB * len(tiles)
    filler = [jnp.zeros((n, r), jnp.float32)] if n else []
    z = jnp.concatenate(([t for t, _ in tiles] + filler) * q, 0).T
    pad = jnp.zeros((SUB, r), jnp.float32)
    z_ref[pl.ds(0, SUB), :] = z[r - SUB :] if wrap else pad
    z_ref[pl.ds(SUB, r), :] = z
    z_ref[pl.ds(SUB + r, SUB), :] = z[:SUB] if wrap else pad
    place = lane((plan.devices, r)) // SUB
    out = jnp.zeros((plan.devices, r), jnp.float32)
    for i in range(q):
        loads = {}
        for k, (_, offsets) in enumerate(tiles):
            if offsets is None or offsets[i] is None:
                continue
            if offsets[i] not in loads:
                loads[offsets[i]] = z_ref[pl.ds(SUB + i + offsets[i], plan.devices, stride=q), :]
            out = jnp.where(place == i * (plan.width // SUB) + k, loads[offsets[i]], out)
    if sums is not None:
        parts = [z[SUB * i : SUB * i + SUB] for i in range(r // SUB)]
        while len(parts) > 1:
            parts = [x + y for x, y in zip(parts[::2], parts[1::2])]
        whole = jnp.broadcast_to(jnp.sum(parts[0], axis=0, keepdims=True), out.shape)
        out = jnp.where(place == sums, whole, out)
    return out if row is None else out + row


def sent_field(plan, y):
    q = plan.piece
    return [(y, (0,) * q), (y, (-1,) + (None,) * (q - 2) + (1,))]


def receive(plan, got, z_ref):
    for i in range(plan.piece):
        z_ref[pl.ds(i, plan.devices, stride=plan.piece), :] = got
    t = z_ref[...].T
    pos = lane() % plan.piece
    tiles = []
    for k in range(4):
        at = SUB * k
        tile = t[at : at + SUB]
        for i in range(1, plan.piece):
            tile = jnp.where(pos == i, t[i * plan.width + at : i * plan.width + at + SUB], tile)
        tiles.append(tile)
    return tiles


def wrapped(plan, x):
    q, r = plan.piece, plan.rows
    me = lax.axis_index(AXIS)
    at = lane()
    pos = at % q
    later = jnp.where(at == 0, 0.0, pltpu.roll(x, q, 1))
    sooner = jnp.where(at == r - 1, 0.0, pltpu.roll(x, r - q, 1))
    first = jnp.where(me == 0, later, x)
    last = jnp.where(me == plan.devices - 1, sooner, x)
    return jnp.where(pos == 0, first, jnp.where(pos == q - 1, last, 0.0))


def near_levels(plan, v, coef):
    r = plan.rows
    at = lane()
    for k in plan.near:
        s = 2**k
        turned = [pltpu.roll(x, s, 1) for x in v]
        back = [pltpu.roll(x, r - s, 1) for x in v]
        lower = [turned[0]] + [jnp.where(at < s, turned[t - 1], turned[t]) for t in (1, 2)]
        upper = [jnp.where(at >= r - s, back[t + 1], back[t]) for t in (0, 1)] + [back[2]]
        fresh = list(v)
        for t in (0, 1, 2) if k < plan.sent else (1,):
            sums = [None] * 4
            for b in range(SUB):
                for side, x in enumerate((lower[t], upper[t])):
                    term = coef(t, side, k, b) * spread(x, b)
                    at_sum = 2 * side + b % 2
                    sums[at_sum] = term if sums[at_sum] is None else sums[at_sum] + term
            fresh[t] = v[t] + (sums[0] + sums[1]) + (sums[2] + sums[3])
        v = fresh
    return v[1]


def square_tile(u):
    return jnp.where(sub() == 0, jnp.broadcast_to(total(u * u), u.shape), 0.0)


def load_kernel(plan, *refs):
    count = (len(refs) - 3) // 2
    ins, outs, edge_refs, sems = refs[:count], refs[count:-3], refs[-3:-1], refs[-1]
    copies = [pltpu.make_async_copy(x, y, sems.at[i]) for i, (x, y) in enumerate(zip(ins, outs))]
    for c in copies:
        c.start()
    for c in copies:
        c.wait()
    rhs_ref, lo_ref, up_ref = outs[:3]
    n = 64 * (plan.sent - 1)
    odd = lax.rem(lax.axis_index(AXIS), 2) == 1
    first = lane((64, plan.rows)) < plan.rows // 2
    low = lo_ref[pl.ds(n, 64), :]
    high = pltpu.roll(up_ref[pl.ds(n, 64), :], plan.rows // 2, 1)
    as_prev, as_next = jnp.where(first, high, low), jnp.where(first, low, high)
    across_ref, pair_ref = edge_refs
    across_ref[pl.ds(2 * n, 64), :] = jnp.where(odd, as_prev, as_next)
    pair_ref[pl.ds(2 * n, 64), :] = jnp.where(odd, as_next, as_prev)
    for ref in edge_refs:
        ref[pl.ds(0, n), :] = lo_ref[pl.ds(0, n), :]
        ref[pl.ds(n, n), :] = up_ref[pl.ds(0, n), :]
        ref[pl.ds(2 * n + 64, SUB), :] = rhs_ref[...]


def take_kernel(in_ref, out_ref):
    out_ref[...] = in_ref[...]


def pack_kernel(plan, first, last, lo_ref, up_ref, fin_ref, dia_ref, bel_ref, abo_ref, out_ref, z_ref):
    half = lax.axis_index(AXIS) >= plan.devices // 2
    *most, top = plan.far
    mats = [(lo_ref, 64 * k) for k in most] + [(up_ref, 64 * k) for k in most] + [None]
    mats += [(fin_ref, 0), (dia_ref, 0), (bel_ref, 0), (abo_ref, 0)]

    def raw(index):
        mat, b = divmod(index, SUB)
        if mats[mat] is None:
            low, high = (ref[pl.ds(64 * top + b, SUB, stride=SUB), :] for ref in (lo_ref, up_ref))
            return jnp.where(half, low, high)
        ref, base = mats[mat]
        return ref[pl.ds(base + b, SUB, stride=SUB), :]

    def tile(index):
        if index < plan.own_tiles:
            return raw(index)
        if index >= plan.coef_tiles:
            return jnp.zeros((SUB, plan.rows), jnp.float32)
        q, r = plan.piece, plan.rows
        even = lane() // q % 2 == 0
        out = None
        for m in range(q):
            x = raw(q * (index - plan.own_tiles) + m)
            x = jnp.where(even, pltpu.roll(x, m + 1, 1), pltpu.roll(x, r - q + m, 1))
            out = x if out is None else jnp.where(lane() % q == m, x, out)
        return out

    t = plan.per_group
    rows = out_ref.shape[0] // plan.devices
    for slot, g in enumerate(range(first, last)):
        z_ref[slot] = jnp.concatenate([tile(g * t + i) for i in range(t)], 0).T
        for i in range(plan.piece):
            out_ref[pl.ds(slot * plan.piece + i, plan.devices, stride=rows), :] = z_ref[
                slot, pl.ds(i, plan.devices, stride=plan.piece), :
            ]


def first_kernel(
    plan, lo_ref, up_ref, rhs_ref, pair_ref, other_ref, late_ref, out_ref, coef_ref, field_ref, z_ref, row_ref, sem
):
    last = plan.sent - 1
    n = 64 * (2 * last + 1)
    odd = lax.rem(lax.axis_index(AXIS), 2) == 1
    rhs = rhs_ref[...]

    def halo(t, start, stride):
        a, b = pair_ref[pl.ds(start, SUB, stride=stride), :], other_ref[pl.ds(start, SUB, stride=stride), :]
        return jnp.where(odd, a, b) if t == 0 else jnp.where(odd, b, a)

    def coef(t, side, k, b):
        if t == 1:
            ref = up_ref if side else lo_ref
            x = ref[pl.ds(64 * k + b, SUB, stride=SUB), :]
        elif k < last:
            x = halo(t, 64 * (last * side + k) + b, SUB)
        else:
            x = halo(t, 64 * 2 * last + b, SUB)
            x = pltpu.roll(x, plan.rows // 2, 1) if side else x
        coef_ref[t, side, k, b] = x
        return x

    fields = [halo(0, n, 1), rhs, halo(2, n, 1)]
    for t in range(3):
        field_ref[t] = fields[t]
    y = near_levels(plan, fields, coef)
    plain = (0,) * plan.piece
    row = send(plan, [*sent_field(plan, y), (square_tile(rhs), plain), (rhs, plain)], z_ref, wrap=True)
    for i in range(plan.devices):
        row_ref[i] = row[i : i + 1]
    copy = pltpu.make_async_copy(row_ref, out_ref.at[:, plan.late_rows - 1], sem)
    copy.start()
    copy.wait()


def far_stage(plan, own, halo, coef_ref):
    q, r, n = plan.piece, plan.rows, len(plan.far) - 1
    base = plan.own_tiles

    def apply(mat, x, start):
        return added([coef_ref[start + mat * SUB + b] * spread(x, b) for b in range(SUB)])

    for k in range(n):
        by = q * 2**k
        fresh = []
        for x, start in ((own, 0), (halo, base)):
            low = apply(k, pltpu.roll(x, by, 1), start)
            high = apply(n + k, pltpu.roll(x, r - by, 1), start)
            fresh.append(x + low + high)
        own, halo = fresh
    own, halo = (x + apply(2 * n, pltpu.roll(x, r // 2, 1), start) for x, start in ((own, 0), (halo, base)))
    own = own + apply(2 * n + 1, own, 0)
    halo = wrapped(plan, halo + apply(2 * n + 1, halo, base))
    pos = lane() % q
    before = jnp.where(pos == 0, halo, pltpu.roll(own, 1, 1))
    after = jnp.where(pos == q - 1, halo, pltpu.roll(own, r - 1, 1))
    w = 2.0 * own + apply(2 * n + 2, own, 0)
    return w + apply(2 * n + 3, before, 0) + apply(2 * n + 4, after, 0)


def norm_of(plan, squares):
    pos = lane() % plan.piece
    one = jnp.where((pos == 0) & (sub() == 0), squares, 0.0)
    return jnp.sqrt(jnp.broadcast_to(total(one), one.shape) / plan.count + EPS)


def finish_far(plan, y, halo, s, vs, coef_ref, z_ref, out_ref):
    w = far_stage(plan, y, halo, coef_ref) / s
    q = plan.piece
    dots = jnp.zeros_like(w)
    for i, v in enumerate(vs):
        dots = jnp.where(sub() == i, jnp.sum(v * w, axis=0, keepdims=True), dots)
    tiles = [(w, (by,) * q) for by in (-q, 0, q)] + [(dots, None)]
    out_ref[...] = send(plan, tiles, z_ref, sums=3)
    return w


def two_sum(a, b):
    s = a + b
    t = s - a
    return s, (a - (s - t)) + (b - t)


def halves(a):
    c = 4097.0 * a
    hi = c - (c - a)
    return hi, a - hi


def two_prod(a, b):
    p = a * b
    ah, al = halves(a)
    bh, bl = halves(b)
    return p, ((ah * bh - p) + ah * bl + al * bh) + al * bl


def pair_add(x, y):
    s, e = two_sum(x[0], y[0])
    e = e + (x[1] + y[1])
    hi = s + e
    return hi, e - (hi - s)


def pair_mul(x, y):
    p, e = two_prod(x[0], y[0])
    e = e + (x[0] * y[1] + x[1] * y[0])
    hi = p + e
    return hi, e - (hi - p)


def folded(x, shifts, axis):
    for s in shifts:
        x = pair_add(x, tuple(pltpu.roll(a, s, axis) for a in x))
    return x


def products():
    out = [(i, None) for i in range(ITERS)] + [(None, None)]
    return out + [(i, j) for i in range(ITERS) for j in range(i, ITERS)]


def rows_sum(pair):
    parts = [tuple(x[SUB * i : SUB * i + SUB] for x in pair) for i in range(pair[0].shape[0] // SUB)]
    while len(parts) > 1:
        half = len(parts) // 2
        parts = [pair_add(a, b) for a, b in zip(parts[:half], parts[half:])]
    one = folded(parts[0], (4, 2, 1), 0)
    return tuple(x[0:1] for x in one)


def last_far_kernel(plan, in_ref, coef_ref, h_ref, w_in_ref, *rest):
    j = ITERS - 1
    vs = [v[...] for v in rest[:j]]
    out_ref, s_ref, zr_ref, zs_ref = rest[j:]
    y, halo, s, v = enter_far(plan, in_ref, h_ref, w_in_ref, vs, zr_ref)
    s_ref[...] = s
    vs = vs + [v]
    w = far_stage(plan, y, halo, coef_ref) / s
    at = sub((2 * SUB, plan.rows))
    packed = [jnp.zeros((2 * SUB, plan.rows), jnp.float32)] * 2
    for i, (a, b) in enumerate(products()):
        pair = two_prod(w if a is None else vs[a], w if b is None else vs[b])
        pair = folded(pair, (4, 2, 1), 0)
        packed = [jnp.where(at == i, jnp.concatenate([x, x], 0), old) for x, old in zip(pair, packed)]
    filler = jnp.zeros((plan.rows - 2 * SUB, plan.rows), jnp.float32)
    hi, lo = rows_sum(tuple(jnp.concatenate([x, filler], 0).T for x in packed))
    hi, lo = (jnp.concatenate([x] * SUB, 0) for x in (hi, lo))
    row = pltpu.roll(hi, SUB, 1) + pltpu.roll(lo, SUB + len(products()), 1)
    out_ref[...] = send(plan, [(w, (0,) * plan.piece)], zs_ref, row=row[0:1])


def unpack(plan, groups, in_ref, rows, coef_ref, z_ref, lent_ref=None):
    q, r = plan.piece, plan.rows
    at = lane()
    n = len(plan.far) - 1
    even = lax.rem(lax.axis_index(AXIS), 2) == 0
    outer = jnp.where(even, (at % q == 0).astype(jnp.int32), (at % q == q - 1).astype(jnp.int32)) == 1

    def limited(x, mat):
        if mat < n:
            return jnp.where(at < q * 2**mat, 0.0, x)
        if mat < 2 * n:
            return jnp.where(at >= r - q * 2 ** (mat - n), 0.0, x)
        return x

    def moved(x, by):
        return pltpu.roll(x, by % r, 1) if by % r else x

    for slot, g in enumerate(groups):
        for i in range(q):
            z_ref[slot, pl.ds(i, plan.devices, stride=q), :] = in_ref[
                pl.ds(slot * q + i, plan.devices, stride=rows), :
            ]
        t = z_ref[slot].T
        for j in range(plan.per_group):
            index = g * plan.per_group + j
            tile = t[SUB * j : SUB * j + SUB]
            if index < plan.own_tiles:
                coef_ref[index] = limited(tile, index // SUB)
            elif index < plan.coef_tiles:
                for m in range(q):
                    k = q * (index - plan.own_tiles) + m
                    x = jnp.where(even, moved(tile, -m), moved(tile, q - 1 - m))
                    coef_ref[plan.own_tiles + k] = jnp.where(outer, limited(x, k // SUB), lent_ref[k])


def unpack_kernel(plan, early_ref, coef_ref, lend_ref, z_ref):
    unpack(plan, range(plan.early), early_ref, plan.early_rows, coef_ref, z_ref)
    even = lax.rem(lax.axis_index(AXIS), 2) == 0
    by = plan.piece - 1
    for k in range(plan.halo_tiles):
        x = coef_ref[k]
        lend_ref[k] = jnp.where(even, pltpu.roll(x, plan.rows - by, 1), pltpu.roll(x, by, 1)) if by else x


def start_far_kernel(
    plan, late_ref, early_coef_ref, lent_ref, out_ref, coef_ref, w_ref, v_ref, s_ref, z_ref, zr_ref, zs_ref
):
    unpack(plan, range(plan.early, plan.groups), late_ref, plan.late_rows, coef_ref, z_ref, lent_ref)
    got = late_ref[pl.ds(plan.late_rows - 1, plan.devices, stride=plan.late_rows), :]
    y, halo, squares, rhs = receive(plan, got, zr_ref)
    s = norm_of(plan, squares)
    v = rhs / s
    v_ref[...] = v
    s_ref[...] = s
    w_ref[...] = finish_far(plan, y, halo, s, [v], coef_ref, zs_ref, out_ref)


def near_kernel(plan, j, in_ref, coef_ref, field_ref, *rest):
    us, ss = rest[: j - 1], rest[j - 1 : 2 * j - 1]
    out_ref, u_ref, h_ref, zr_ref, zs_ref = rest[2 * j - 1 :]
    got = in_ref[...]
    dots = jnp.sum(got, axis=0, keepdims=True) / plan.count
    h = [jnp.broadcast_to(dots[:, 3 * SUB + i : 3 * SUB + i + 1], (SUB, plan.rows)) for i in range(j)]
    w = receive(plan, got, zr_ref)[:3]
    tall = jnp.zeros_like(h[0])
    for i in range(j):
        tall = jnp.where(sub() == i, h[i], tall)
    h_ref[...] = tall
    fields = [field_ref, *us]
    for t in range(3):
        acc = None
        for i in range(j):
            term = h[i] * (fields[i][t] / ss[i][...])
            acc = term if acc is None else acc + term
        w[t] = w[t] - acc
        u_ref[t] = w[t]
    y = near_levels(plan, w, lambda t, side, k, b: coef_ref[t, side, k, b])
    out_ref[...] = send(plan, [*sent_field(plan, y), (square_tile(w[1]), (0,) * plan.piece)], zs_ref, wrap=True)


def enter_far(plan, in_ref, h_ref, w_in_ref, vs, z_ref):
    y, halo, squares, _ = receive(plan, in_ref[...], z_ref)
    s = norm_of(plan, squares)
    h = h_ref[...]
    acc = None
    for i, v in enumerate(vs):
        term = spread(h, i) * v
        acc = term if acc is None else acc + term
    return y, halo, s, (w_in_ref[...] - acc) / s


def far_kernel(plan, j, in_ref, coef_ref, h_ref, w_in_ref, *rest):
    vs = [v[...] for v in rest[:j]]
    out_ref, w_ref, v_ref, s_ref, zr_ref, zs_ref = rest[j:]
    y, halo, s, v = enter_far(plan, in_ref, h_ref, w_in_ref, vs, zr_ref)
    v_ref[...] = v
    s_ref[...] = s
    w_ref[...] = finish_far(plan, y, halo, s, vs + [v], coef_ref, zs_ref, out_ref)


def output_kernel(plan, in_ref, field_ref, *rest):
    us = rest[: ITERS - 1]
    ss = [s[...] for s in rest[ITERS - 1 : 2 * ITERS - 1]]
    hs = [h[...] for h in rest[2 * ITERS - 1 : 3 * ITERS - 2]]
    basis_ref, hess_ref, z_ref = rest[3 * ITERS - 2 :]
    raw = in_ref[...]
    low = pltpu.roll(raw, plan.rows - len(products()), 1)
    row = rows_sum((raw, low))
    w = receive(plan, in_ref[...], z_ref)[0]
    wide = lambda x: jnp.broadcast_to(x, (SUB, plan.rows))
    sums = [tuple(wide(x[:, SUB + i : SUB + i + 1]) for x in row) for i in range(len(products()))]
    names = products()
    got = dict(zip(names, sums))
    h = [got[i, None][0] / plan.count for i in range(ITERS)]
    zero = jnp.zeros_like(h[0])
    squares = got[None, None]
    for i in range(ITERS):
        left = tuple(2.0 * x for x in got[i, None])
        for j in range(ITERS):
            left = pair_add(left, pair_mul((-h[j], zero), got[min(i, j), max(i, j)]))
        squares = pair_add(squares, pair_mul((-h[i], zero), left))
    squares = jnp.maximum(squares[0], 0.0)
    ss.append(jnp.sqrt(squares / plan.count + EPS))
    fields = [field_ref[1]] + [u[1] for u in us]
    vs = [f / s for f, s in zip(fields, ss)]
    acc = None
    for i in range(ITERS):
        term = h[i] * vs[i]
        acc = term if acc is None else acc + term
    vs.append((w - acc) / ss[-1])
    for j in range(ITERS + 1):
        basis_ref[j] = vs[j]
    top = jnp.zeros_like(w)
    for i in range(ITERS):
        top = jnp.where(sub() == i, h[i], top)
    hs.append(top)
    hess = jnp.zeros_like(w)
    for j in range(ITERS):
        col = jnp.where(sub() <= j, hs[j], jnp.where(sub() == j + 1, ss[j + 1], 0.0))
        hess = jnp.where(lane() == j, col, hess)
    hess_ref[...] = hess[: ITERS + 1, :ITERS]


def transposed(
    plan, right_side, diag_block, below_block, above_block, lower_level, upper_level, final_block
):
    r, d = plan.rows, plan.devices
    flat = lambda x: x.reshape(-1, r)
    lo, up, fin = flat(lower_level), flat(upper_level), flat(final_block)
    dia, bel, abo = flat(diag_block), flat(below_block), flat(above_block)
    shape = lambda *s: jax.ShapeDtypeStruct(s, jnp.float32)
    tile = shape(SUB, r)
    scratch = lambda *s: pltpu.VMEM(s, jnp.float32)

    def call(kernel, outs, scratches, *args, space=pltpu.VMEM, flops=1_000_000, places=None, out_places=None, **more):
        return pl.pallas_call(
            kernel,
            out_shape=outs,
            in_specs=[pl.BlockSpec(memory_space=x) for x in places or [space] * len(args)],
            out_specs=jax.tree.map(lambda _: pl.BlockSpec(memory_space=pltpu.VMEM), outs)
            if out_places is None
            else [pl.BlockSpec(memory_space=x) for x in out_places],
            scratch_shapes=scratches,
            compiler_params=pltpu.CompilerParams(vmem_limit_bytes=24 * 2**20),
            cost_estimate=pl.CostEstimate(flops=flops, bytes_accessed=1_000_000, transcendentals=0),
            **more,
        )(*args)

    def exchange(x):
        y = lax.all_to_all(x.reshape(-1, 1, r), AXIS, 0, 0, tiled=True)
        return y.reshape(-1, r)

    part = functools.partial
    raw = tuple(pltpu.with_memory_space_constraint(x, pltpu.HBM) for x in (right_side, lo, up, fin, dia, bel, abo))
    edge = shape(64 * (2 * plan.sent - 1) + SUB, r)
    *loaded, edge_across, edge_pair = call(
        part(load_kernel, plan),
        (*(shape(*x.shape) for x in raw), edge, edge),
        [pltpu.SemaphoreType.DMA((len(raw),))],
        *raw,
        space=pltpu.HBM,
    )
    rhs, lo, up = loaded[:3]
    mats = loaded[1:]
    other = lax.ppermute(edge_across, AXIS, [(i, i + 1 if i % 2 else i - 1) for i in range(1, d - 1)])
    pair = lax.ppermute(edge_pair, AXIS, [(i, i ^ 1) for i in range(d)])
    pair = call(take_kernel, edge, [], pair)
    early = call(
        part(pack_kernel, plan, 0, plan.early),
        shape(d * plan.early_rows, r),
        [scratch(plan.early, r, r)],
        *mats,
        flops=10_000_000,
    )
    early = exchange(early)
    late_shape = shape(d * plan.late_rows, r)
    late = call(
        part(pack_kernel, plan, plan.early, plan.groups),
        late_shape,
        [scratch(plan.groups - plan.early, r, r)],
        *mats,
        flops=10_000_000,
    )
    late_shape = shape(d, plan.late_rows, 1, r)
    late, near, fields = call(
        part(first_kernel, plan),
        (late_shape, shape(3, 2, len(plan.near), SUB, SUB, r), shape(3, SUB, r)),
        [scratch(r + 2 * SUB, r), scratch(d, 1, r), pltpu.SemaphoreType.DMA],
        lo, up, rhs, pair, other, late.reshape(late_shape.shape),
        places=[pltpu.VMEM] * 5 + [pl.ANY],
        out_places=[pl.ANY] + [pltpu.VMEM] * 2,
        input_output_aliases={5: 0},
    )
    small = shape(d, r)
    padded = scratch(r + 2 * SUB, r)
    two = [scratch(r, r), padded]
    late = exchange(late)
    coef_shape = shape(plan.own_tiles + plan.halo_tiles, SUB, r)
    lend_shape = shape(plan.halo_tiles, SUB, r)
    coef, lent = call(
        part(unpack_kernel, plan), (coef_shape, lend_shape), [scratch(plan.early, r, r)], early, flops=5_000_000
    )
    lent = lax.ppermute(lent, AXIS, [(i, i ^ 1) for i in range(d)])
    out, coef, w, v, s = call(
        part(start_far_kernel, plan),
        (small, coef_shape, tile, tile, tile),
        [scratch(plan.groups - plan.early, r, r), *two],
        late, coef, lent,
        input_output_aliases={1: 1},
    )
    us, ss, vs, hs = [], [s], [v], []
    for j in range(1, ITERS):
        out, u, h = call(
            part(near_kernel, plan, j),
            (small, shape(3, SUB, r), tile),
            two,
            exchange(out), near, fields, *us, *ss,
        )
        us.append(u)
        hs.append(h)
        if j < ITERS - 1:
            out, w, v, s = call(
                part(far_kernel, plan, j), (small, tile, tile, tile), two, exchange(out), coef, h, w, *vs
            )
            vs.append(v)
        else:
            out, s = call(part(last_far_kernel, plan), (small, tile), two, exchange(out), coef, h, w, *vs)
        ss.append(s)
    return call(
        part(output_kernel, plan),
        (shape(ITERS + 1, SUB, r), shape(ITERS + 1, ITERS)),
        [scratch(r, r)],
        exchange(out), fields, *us, *ss, *hs,
    )


def on_device(*args):
    right_side, lower_level = args[0], args[4]
    devices, rows = lax.axis_size(AXIS), right_side.shape[1]
    if not fits(devices, rows, right_side.shape[0]):
        return general(*args)
    return tuple(transposed(Plan(devices, rows, lower_level.shape[0]), *args))


def solution(mesh):
    return jax.shard_map(
        on_device,
        mesh=mesh,
        in_specs=(
            P(None, "chain"),
            P(None, None, "chain"),
            P(None, None, "chain"),
            P(None, None, "chain"),
            P(None, None, None, "chain"),
            P(None, None, None, "chain"),
            P(None, None, "chain"),
        ),
        out_specs=(P(None, None, "chain"), P()),
        check_vma=False,
    )
```

profile of v0, /device:TPU:0, one launch (start us, length us, event | category | flops | bytes accessed | tf_op | source)
XLA Modules:
  0.0 90.2 jit_solution(18008634063587212307)
XLA Ops:
  0.6 1.3 %shard_map.86 = (f32[8,128]{1,0:T(8,128)S(1)}, f32[768,128]{1,0:T(8,128)S(1)}, f32[768,128]{1,0:T(8,128)S(1)}, f32[64,128]{1,0:T(8,128)S(1)}, f32[64,128]{1,0:T(...) custom-call(f32[8,128]{1,0:T(8,128)} %refs_0_.1, ...), custom_call_target="tpu_custom_call" | custom-call | flops 1000000 | bytes 1000000 | tf_op jit(solution)/shard_map/pallas_call | solution.py:610
  1.9 0.9 %shard_map.90 = f32[640,128]{1,0:T(8,128)} custom-call(f32[768,128]{1,0:T(8,128)S(1)} %get-tuple-element.33.lo_ref, f32[768,128]{1,0:T(8,128)S(1)} %get-tuple-element.34.up_ref, f32[64,128]{1,0:T(8,128)S(1)} %get-tuple-element.38.fin_ref, f32[64,128]{1,0:T(8,128)S(1)} %get-tuple-element.39.dia_ref, f32[64,128]{1,0:T(8,128)S(1)} %get-tuple-element.40.bel_ref, ...), custom_call_target="tpu_custom_call" | custom-call | flops 10000000 | bytes 1000000 | tf_op jit(solution)/shard_map/pallas_call | solution.py:610
  2.9 7.3 %all-to-all-start.1 = ((f32[640,1,128]{2,1,0:T(1,128)}), f32[640,1,128]{2,1,0:T(1,128)S(1)}, u32[]{:S(2)}, u32[]{:S(2)}) async-start(f32[640,1,128]{2,1,0:T(1,128)} %bitcast.11), calls=%async_computation.1 | async-start | bytes 655360 | tf_op jit(solution)/shard_map/all_to_all | solution.py:624
  10.2 0.3 collective-permute-start
  10.5 0.7 collective-permute-start.1
  11.2 1.1 %shard_map.88 = f32[416,128]{1,0:T(8,128)} custom-call(f32[768,128]{1,0:T(8,128)S(1)} %get-tuple-element.33.lo_ref, f32[768,128]{1,0:T(8,128)S(1)} %get-tuple-element.34.up_ref, f32[64,128]{1,0:T(8,128)S(1)} %get-tuple-element.38.fin_ref, f32[64,128]{1,0:T(8,128)S(1)} %get-tuple-element.39.dia_ref, f32[64,128]{1,0:T(8,128)S(1)} %get-tuple-element.40.bel_ref, ...), custom_call_target="tpu_custom_call" | custom-call | flops 10000000 | bytes 1000000 | tf_op jit(solution)/shard_map/pallas_call | solution.py:610
  12.3 0.0 collective-permute-done.in_ref
  12.3 0.0 collective-permute-done.1.other_ref
  12.3 1.4 %shard_map.89 = (f32[32,13,1,128]{3,2,1,0:T(1,128)}, f32[3,2,7,8,8,128]{5,4,3,2,1,0:T(8,128)S(1)}, f32[3,8,128]{2,1,0:T(8,128)S(1)}) custom-call(f32[768,128]{1,0:T(8,128)S(1)} %get-tuple-element.33.lo_ref, f32[768,128]{1,0:T(8,128)S(1)} %get-tuple-element.34.up_ref, f32[8,128]{1,0:T(8,128)S(1)} %get-tuple-element.35.rhs_ref, ...), custom_call_target="tpu_custom_call", output_to_operand_aliasing={{0}: (5, {})} | custom-call | flops 1000000 | bytes 1000000 | tf_op jit(solution)/shard_map/pallas_call | solution.py:610
  13.7 8.5 %all-to-all-done.1 = f32[640,1,128]{2,1,0:T(1,128)S(1)} async-done(((f32[640,1,128]{2,1,0:T(1,128)}), f32[640,1,128]{2,1,0:T(1,128)S(1)}, u32[]{:S(2)}, u32[]{:S(2)}) %all-to-all-start.1) | async-done | bytes 327712 | tf_op jit(solution)/shard_map/all_to_all | solution.py:624
  22.2 8.6 %all-to-all-start = ((f32[416,1,128]{2,1,0:T(1,128)}), f32[416,1,128]{2,1,0:T(1,128)S(1)}, u32[]{:S(2)}, u32[]{:S(2)}) async-start(f32[416,1,128]{2,1,0:T(1,128)} %bitcast.8), calls=%async_computation | async-start | bytes 425984 | tf_op jit(solution)/shard_map/all_to_all | solution.py:624
  30.9 0.3 shard_map.91
  31.2 0.3 collective-permute-start.2
  31.6 8.8 %all-to-all-done = f32[416,1,128]{2,1,0:T(1,128)S(1)} async-done(((f32[416,1,128]{2,1,0:T(1,128)}), f32[416,1,128]{2,1,0:T(1,128)S(1)}, u32[]{:S(2)}, u32[]{:S(2)}) %all-to-all-start) | async-done | bytes 213024 | tf_op jit(solution)/shard_map/all_to_all | solution.py:624
  40.3 0.0 collective-permute-done.2.lent_ref
  40.3 0.8 shard_map.92
  41.1 9.5 %all_to_all.35 = f32[32,1,128]{2,1,0:T(1,128)S(1)} all-to-all(f32[32,1,128]{2,1,0:T(1,128)S(1)} %bitcast.42), channel_id=1, replica_groups=mesh['chain'=32] {'chain'}, dimensions={0} | all-to-all | bytes 32768 | tf_op jit(solution)/shard_map/all_to_all | solution.py:624
  50.6 0.8 shard_map.93
  51.4 8.9 %all_to_all.36 = f32[32,1,128]{2,1,0:T(1,128)S(1)} all-to-all(f32[32,1,128]{2,1,0:T(1,128)S(1)} %bitcast.46), channel_id=1, replica_groups=mesh['chain'=32] {'chain'}, dimensions={0} | all-to-all | bytes 32768 | tf_op jit(solution)/shard_map/all_to_all | solution.py:624
  60.3 0.7 shard_map.94
  61.0 8.9 %all_to_all.37 = f32[32,1,128]{2,1,0:T(1,128)S(1)} all-to-all(f32[32,1,128]{2,1,0:T(1,128)S(1)} %bitcast.44), channel_id=1, replica_groups=mesh['chain'=32] {'chain'}, dimensions={0} | all-to-all | bytes 32768 | tf_op jit(solution)/shard_map/all_to_all | solution.py:624
  69.8 0.8 shard_map.95
  70.7 8.9 %all_to_all.38 = f32[32,1,128]{2,1,0:T(1,128)S(1)} all-to-all(f32[32,1,128]{2,1,0:T(1,128)S(1)} %bitcast.45), channel_id=1, replica_groups=mesh['chain'=32] {'chain'}, dimensions={0} | all-to-all | bytes 32768 | tf_op jit(solution)/shard_map/all_to_all | solution.py:624
  79.5 0.9 shard_map.96
  80.4 8.9 %all_to_all.39 = f32[32,1,128]{2,1,0:T(1,128)S(1)} all-to-all(f32[32,1,128]{2,1,0:T(1,128)S(1)} %bitcast.43), channel_id=1, replica_groups=mesh['chain'=32] {'chain'}, dimensions={0} | all-to-all | bytes 32768 | tf_op jit(solution)/shard_map/all_to_all | solution.py:624
  89.3 0.9 %shard_map.97 = (f32[4,8,128]{2,1,0:T(8,128)}, f32[4,3]{1,0:T(4,128)}) custom-call(f32[32,128]{1,0:T(8,128)S(1)} %bitcast.41, f32[3,8,128]{2,1,0:T(8,128)S(1)} %get-tuple-element.47.field_ref, f32[3,8,128]{2,1,0:T(8,128)S(1)} %get-tuple-element.55.rest_0_, f32[3,8,128]{2,1,0:T(8,128)S(1)} %get-tuple-element.62.rest_1_, ...), custom_call_target="tpu_custom_call" | custom-call | flops 1000000 | bytes 1000000 | tf_op jit(solution)/shard_map/pallas_call | solution.py:610
  (1 shorter events, 0.0 us)
Async XLA Ops:
  2.9 19.4 %all-to-all-start.1 = ((f32[640,1,128]{2,1,0:T(1,128)}), f32[640,1,128]{2,1,0:T(1,128)S(1)}, u32[]{:S(2)}, u32[]{:S(2)}) async-start(f32[640,1,128]{2,1,0:T(1,128)} %bitcast.11), calls=%async_computation.1 | async-start | bytes 655360 | tf_op jit(solution)/shard_map/all_to_all | solution.py:624
  10.2 2.1 %collective-permute-start = (f32[712,128]{1,0:T(8,128)S(1)}, f32[712,128]{1,0:T(8,128)S(1)}, u32[]{:S(2)}, u32[]{:S(2)}) collective-permute-start(f32[712,128]{1,0:T(8,128)S(1)} %get-tuple-element.36), channel_id=1, source_target_pairs={{0,1},{1,0},{2,3},{3,2},{4,5},{5,4},{6,7},{7,6},{8,9},{9,8},{10,11... | collective-permute-start | bytes 1093640 | tf_op jit(solution)/shard_map/ppermute | solution.py:640
  10.5 1.8 %collective-permute-start.1 = (f32[712,128]{1,0:T(8,128)S(1)}, f32[712,128]{1,0:T(8,128)S(1)}, u32[]{:S(2)}, u32[]{:S(2)}) collective-permute-start(f32[712,128]{1,0:T(8,128)S(1)} %get-tuple-element.37), channel_id=1, source_target_pairs={{1,2},{2,1},{3,4},{4,3},{5,6},{6,5},{7,8},{8,7},{9,10},{10,9},{11,... | collective-permute-start | bytes 1093640 | tf_op jit(solution)/shard_map/ppermute | solution.py:639
  22.2 18.1 %all-to-all-start = ((f32[416,1,128]{2,1,0:T(1,128)}), f32[416,1,128]{2,1,0:T(1,128)S(1)}, u32[]{:S(2)}, u32[]{:S(2)}) async-start(f32[416,1,128]{2,1,0:T(1,128)} %bitcast.8), calls=%async_computation | async-start | bytes 425984 | tf_op jit(solution)/shard_map/all_to_all | solution.py:624
  31.2 9.1 %collective-permute-start.2 = (f32[80,8,128]{2,1,0:T(8,128)S(1)}, f32[80,8,128]{2,1,0:T(8,128)S(1)}, u32[]{:S(2)}, u32[]{:S(2)}) collective-permute-start(f32[80,8,128]{2,1,0:T(8,128)S(1)} %get-tuple-element.44), channel_id=1, source_target_pairs={{0,1},{1,0},{2,3},{3,2},{4,5},{5,4},{6,7},{7,6},{8,9},{9,8},{10,11... | collective-permute-start | bytes 983048 | tf_op jit(solution)/shard_map/ppermute | solution.py:677
where the time goes:
time: 90.6 us; the launch traced here: 90.2 us
  blocking collectives  45 us (50%)
  starting transfers between devices  17.3 us (19%)
  waiting for transfers between devices  17.3 us (19%)
  Pallas kernels  9.91 us (11%)
    all_to_all x5, blocking collectives, exchange(): y = lax.all_to_all(x.reshape(-1, 1, r), AXIS, 0, 0, tiled=True)  45 us
    all_to_all x2, waiting for transfers between devices, exchange(): y = lax.all_to_all(x.reshape(-1, 1, r), AXIS, 0, 0, tiled=True)  17.3 us
    all_to_all x2, starting transfers between devices, exchange(): y = lax.all_to_all(x.reshape(-1, 1, r), AXIS, 0, 0, tiled=True)  16 us
    pallas_call x12, Pallas kernels, call(): pl.pallas_call(kernel, out_shape=outs, in_specs=[pl.BlockSpec(memory_spac...  9.91 us
  transfers between devices with their start and end apart: 5, of which 2 were waited for; matrix products, arithmetic and copies ran while one was open for 0% of the time, Pallas kernels for 3%

commit v1 on v0

--- a/solution.py
+++ b/solution.py
@@ -114,7 +114,7 @@
         self.coef_tiles = self.own_tiles + self.halo_tiles // self.piece
         self.per_group = rows // SUB
         self.groups = -(-self.coef_tiles // self.per_group)
-        self.early = -(-self.halo_tiles // self.per_group)
+        self.early = -(-self.halo_tiles // self.per_group) + 1
         self.early_rows = self.early * self.piece
         self.late_rows = (self.groups - self.early) * self.piece + 1
         self.width = rows // self.piece
@@ -218,13 +218,13 @@
         upper = [jnp.where(at >= r - s, back[t + 1], back[t]) for t in (0, 1)] + [back[2]]
         fresh = list(v)
         for t in (0, 1, 2) if k < plan.sent else (1,):
-            sums = [None] * 4
+            low_sum = high_sum = None
             for b in range(SUB):
-                for side, x in enumerate((lower[t], upper[t])):
-                    term = coef(t, side, k, b) * spread(x, b)
-                    at_sum = 2 * side + b % 2
-                    sums[at_sum] = term if sums[at_sum] is None else sums[at_sum] + term
-            fresh[t] = v[t] + (sums[0] + sums[1]) + (sums[2] + sums[3])
+                low = coef(t, 0, k, b) * spread(lower[t], b)
+                high = coef(t, 1, k, b) * spread(upper[t], b)
+                low_sum = low if low_sum is None else low_sum + low
+                high_sum = high if high_sum is None else high_sum + high
+            fresh[t] = v[t] + low_sum + high_sum
         v = fresh
     return v[1]
 

time: 90.6 us -> 88.9 us (0.981)
  blocking collectives: 45 us -> 58.5 us
  starting transfers between devices: 17.3 us -> 8.38 us
  waiting for transfers between devices: 17.3 us -> 12.3 us
  Pallas kernels: 9.91 us -> 8.66 us
    all_to_all x5 -> x6, blocking collectives: 45 us -> 58.5 us  [exchange(): y = lax.all_to_all(x.reshape(-1, 1, r), AXIS, 0, 0, tiled=True)]
    all_to_all x2 -> x1, starting transfers between devices: 16 us -> 7.33 us  [exchange(): y = lax.all_to_all(x.reshape(-1, 1, r), AXIS, 0, 0, tiled=True)]
    all_to_all x2 -> x1, waiting for transfers between devices: 17.3 us -> 12.2 us  [exchange(): y = lax.all_to_all(x.reshape(-1, 1, r), AXIS, 0, 0, tiled=True)]
    pallas_call x12, Pallas kernels: 9.91 us -> 8.66 us  [call(): pl.pallas_call(kernel, out_shape=outs, in_specs=[pl.BlockSpec(memory_spac...]
  transfers between devices with their start and end apart: 5 -> 4, of which waited for: 2 -> 1; matrix products, arithmetic and copies ran while one was open for 0% -> 0% of each run, Pallas kernels for 3% -> 2%
where the time goes in v1:
time: 88.9 us; the launch traced here: 88.5 us
  blocking collectives  58.5 us (66%)
  waiting for transfers between devices  12.3 us (14%)
  Pallas kernels  8.66 us (10%)
  starting transfers between devices  8.38 us (9%)
    all_to_all x6, blocking collectives, exchange(): y = lax.all_to_all(x.reshape(-1, 1, r), AXIS, 0, 0, tiled=True)  58.5 us
    all_to_all x1, waiting for transfers between devices, exchange(): y = lax.all_to_all(x.reshape(-1, 1, r), AXIS, 0, 0, tiled=True)  12.2 us
    pallas_call x12, Pallas kernels, call(): pl.pallas_call(kernel, out_shape=outs, in_specs=[pl.BlockSpec(memory_spac...  8.66 us
    all_to_all x1, starting transfers between devices, exchange(): y = lax.all_to_all(x.reshape(-1, 1, r), AXIS, 0, 0, tiled=True)  7.33 us
  transfers between devices with their start and end apart: 4, of which 1 were waited for; matrix products, arithmetic and copies ran while one was open for 0% of the time, Pallas kernels for 2%

profile of v1, /device:TPU:0, one launch (start us, length us, event | category | flops | bytes accessed | tf_op | source)
XLA Modules:
  0.0 88.5 jit_solution(9824632254076182553)
XLA Ops:
  0.6 1.3 %shard_map.86 = (f32[8,128]{1,0:T(8,128)S(1)}, f32[768,128]{1,0:T(8,128)S(1)}, f32[768,128]{1,0:T(8,128)S(1)}, f32[64,128]{1,0:T(8,128)S(1)}, f32[64,128]{1,0:T(...) custom-call(f32[8,128]{1,0:T(8,128)} %refs_0_.1, ...), custom_call_target="tpu_custom_call" | custom-call | flops 1000000 | bytes 1000000 | tf_op jit(solution)/shard_map/pallas_call | solution.py:610
  1.9 0.9 %shard_map.90 = f32[768,128]{1,0:T(8,128)} custom-call(f32[768,128]{1,0:T(8,128)S(1)} %get-tuple-element.33.lo_ref, f32[768,128]{1,0:T(8,128)S(1)} %get-tuple-element.34.up_ref, f32[64,128]{1,0:T(8,128)S(1)} %get-tuple-element.38.fin_ref, f32[64,128]{1,0:T(8,128)S(1)} %get-tuple-element.39.dia_ref, f32[64,128]{1,0:T(8,128)S(1)} %get-tuple-element.40.bel_ref, ...), custom_call_target="tpu_custom_call" | custom-call | flops 10000000 | bytes 1000000 | tf_op jit(solution)/shard_map/pallas_call | solution.py:610
  2.9 7.3 %all-to-all-start.1 = ((f32[768,1,128]{2,1,0:T(1,128)}), f32[768,1,128]{2,1,0:T(1,128)S(1)}, u32[]{:S(2)}, u32[]{:S(2)}) async-start(f32[768,1,128]{2,1,0:T(1,128)} %bitcast.11), calls=%async_computation.1 | async-start | bytes 786432 | tf_op jit(solution)/shard_map/all_to_all | solution.py:624
  10.2 0.3 collective-permute-start
  10.5 0.7 collective-permute-start.1
  11.2 12.2 %all-to-all-done.1 = f32[768,1,128]{2,1,0:T(1,128)S(1)} async-done(((f32[768,1,128]{2,1,0:T(1,128)}), f32[768,1,128]{2,1,0:T(1,128)S(1)}, u32[]{:S(2)}, u32[]{:S(2)}) %all-to-all-start.1) | async-done | bytes 393248 | tf_op jit(solution)/shard_map/all_to_all | solution.py:624
  23.5 0.4 shard_map.91
  23.8 0.1 collective-permute-start.2
  23.9 0.4 shard_map.88
  24.3 0.0 collective-permute-done.in_ref
  24.3 0.0 collective-permute-done.1.other_ref
  24.3 0.8 shard_map.89
  25.1 13.9 %all_to_all.35 = f32[288,1,128]{2,1,0:T(1,128)S(1)} all-to-all(f32[288,1,128]{2,1,0:T(1,128)S(1)} %bitcast.37), channel_id=1, replica_groups=mesh['chain'=32] {'chain'}, dimensions={0} | all-to-all | bytes 294912 | tf_op jit(solution)/shard_map/all_to_all | solution.py:624
  39.0 0.0 collective-permute-done.2.lent_ref
  39.0 0.8 shard_map.92
  39.8 9.1 %all_to_all.36 = f32[32,1,128]{2,1,0:T(1,128)S(1)} all-to-all(f32[32,1,128]{2,1,0:T(1,128)S(1)} %bitcast.44), channel_id=1, replica_groups=mesh['chain'=32] {'chain'}, dimensions={0} | all-to-all | bytes 32768 | tf_op jit(solution)/shard_map/all_to_all | solution.py:624
  48.9 0.8 shard_map.93
  49.7 8.9 %all_to_all.37 = f32[32,1,128]{2,1,0:T(1,128)S(1)} all-to-all(f32[32,1,128]{2,1,0:T(1,128)S(1)} %bitcast.48), channel_id=1, replica_groups=mesh['chain'=32] {'chain'}, dimensions={0} | all-to-all | bytes 32768 | tf_op jit(solution)/shard_map/all_to_all | solution.py:624
  58.6 0.7 shard_map.94
  59.3 8.9 %all_to_all.38 = f32[32,1,128]{2,1,0:T(1,128)S(1)} all-to-all(f32[32,1,128]{2,1,0:T(1,128)S(1)} %bitcast.46), channel_id=1, replica_groups=mesh['chain'=32] {'chain'}, dimensions={0} | all-to-all | bytes 32768 | tf_op jit(solution)/shard_map/all_to_all | solution.py:624
  68.2 0.8 shard_map.95
  69.0 8.9 %all_to_all.39 = f32[32,1,128]{2,1,0:T(1,128)S(1)} all-to-all(f32[32,1,128]{2,1,0:T(1,128)S(1)} %bitcast.47), channel_id=1, replica_groups=mesh['chain'=32] {'chain'}, dimensions={0} | all-to-all | bytes 32768 | tf_op jit(solution)/shard_map/all_to_all | solution.py:624
  77.9 0.9 shard_map.96
  78.7 8.9 %all_to_all.40 = f32[32,1,128]{2,1,0:T(1,128)S(1)} all-to-all(f32[32,1,128]{2,1,0:T(1,128)S(1)} %bitcast.45), channel_id=1, replica_groups=mesh['chain'=32] {'chain'}, dimensions={0} | all-to-all | bytes 32768 | tf_op jit(solution)/shard_map/all_to_all | solution.py:624
  87.6 0.9 %shard_map.97 = (f32[4,8,128]{2,1,0:T(8,128)}, f32[4,3]{1,0:T(4,128)}) custom-call(f32[32,128]{1,0:T(8,128)S(1)} %bitcast.43, f32[3,8,128]{2,1,0:T(8,128)S(1)} %get-tuple-element.47.field_ref, f32[3,8,128]{2,1,0:T(8,128)S(1)} %get-tuple-element.55.rest_0_, f32[3,8,128]{2,1,0:T(8,128)S(1)} %get-tuple-element.62.rest_1_, ...), custom_call_target="tpu_custom_call" | custom-call | flops 1000000 | bytes 1000000 | tf_op jit(solution)/shard_map/pallas_call | solution.py:610
  (1 shorter events, 0.0 us)
Async XLA Ops:
  2.9 20.6 %all-to-all-start.1 = ((f32[768,1,128]{2,1,0:T(1,128)}), f32[768,1,128]{2,1,0:T(1,128)S(1)}, u32[]{:S(2)}, u32[]{:S(2)}) async-start(f32[768,1,128]{2,1,0:T(1,128)} %bitcast.11), calls=%async_computation.1 | async-start | bytes 786432 | tf_op jit(solution)/shard_map/all_to_all | solution.py:624
  10.2 14.1 %collective-permute-start = (f32[712,128]{1,0:T(8,128)S(1)}, f32[712,128]{1,0:T(8,128)S(1)}, u32[]{:S(2)}, u32[]{:S(2)}) collective-permute-start(f32[712,128]{1,0:T(8,128)S(1)} %get-tuple-element.36), channel_id=1, source_target_pairs={{0,1},{1,0},{2,3},{3,2},{4,5},{5,4},{6,7},{7,6},{8,9},{9,8},{10,11... | collective-permute-start | bytes 1093640 | tf_op jit(solution)/shard_map/ppermute | solution.py:640
  10.5 13.8 %collective-permute-start.1 = (f32[712,128]{1,0:T(8,128)S(1)}, f32[712,128]{1,0:T(8,128)S(1)}, u32[]{:S(2)}, u32[]{:S(2)}) collective-permute-start(f32[712,128]{1,0:T(8,128)S(1)} %get-tuple-element.37), channel_id=1, source_target_pairs={{1,2},{2,1},{3,4},{4,3},{5,6},{6,5},{7,8},{8,7},{9,10},{10,9},{11,... | collective-permute-start | bytes 1093640 | tf_op jit(solution)/shard_map/ppermute | solution.py:639
  23.8 15.2 %collective-permute-start.2 = (f32[80,8,128]{2,1,0:T(8,128)S(1)}, f32[80,8,128]{2,1,0:T(8,128)S(1)}, u32[]{:S(2)}, u32[]{:S(2)}) collective-permute-start(f32[80,8,128]{2,1,0:T(8,128)S(1)} %get-tuple-element.44), channel_id=1, source_target_pairs={{0,1},{1,0},{2,3},{3,2},{4,5},{5,4},{6,7},{7,6},{8,9},{9,8},{10,11... | collective-permute-start | bytes 983048 | tf_op jit(solution)/shard_map/ppermute | solution.py:677
